TPU v7x, 16 devices: a whole 2x2x2 slice. The times are simulated.
16 devices in a mesh: dp: 4 (over z, y), ep: 4 (over x, core).
Axes of the slice: x: 2, y: 2, z: 2, core: 2. Of those that a mesh axis runs over, the one named last changes fastest.
Arguments:
- w_gate: bfloat16 [1, 8, 4096, 1536], P(None, 'ep')
- w_up: bfloat16 [1, 8, 4096, 1536], P(None, 'ep')
- w_down: bfloat16 [1, 8, 1536, 4096], P(None, 'ep')
- place: int32 [1, 32], replicated
Outputs:
- output 1: bfloat16 [1, 32, 4096, 3072], P(None, ('dp', 'ep'))
- output 2: bfloat16 [1, 32, 1536, 4096], P(None, ('dp', 'ep'))
All inputs are finite; a program needn't handle non-finite values.
Results may differ from a plain program's by a relative error of at most 0.001.
Values are sent between devices in bfloat16 or wider.
A program may use at most 1 GiB of HBM per device.

v0:
```python
import jax
import jax.numpy as jnp
import numpy as np
from jax import lax
from jax.sharding import PartitionSpec as P


def _routes(dp, ep, slots):
    n_dev = dp * ep
    out = []
    for j in range(slots):
        pairs, send_to, local = [], list(range(n_dev)), [False] * n_dev
        for a in range(dp):
            for g in range(ep):
                h = (2 * a - g) % ep if j < ((a + 1) * slots) // dp else (g + j + 1) % ep
                n = a * ep + g
                if h == g:
                    local[n] = True
                    continue
                src = ((a + j) % dp) * ep + h
                pairs.append((src, n))
                send_to[src] = n
        out.append((pairs, send_to, local))
    return out


def solution(mesh):
    dp = mesh.shape["dp"]
    ep = mesh.shape["ep"]
    n_dev = dp * ep

    def body(w_gate, w_up, w_down, place):
        g = lax.axis_index("ep")
        me = lax.axis_index("dp") * ep + g
        n_exp = w_gate.shape[1]
        slots = place.shape[1] // n_dev
        routes = _routes(dp, ep, slots)
        take = jax.vmap(lambda w, i: w[i])
        own = jnp.clip(lax.dynamic_slice_in_dim(place, me * slots, slots, axis=1) - g * n_exp, 0, n_exp - 1)
        own13 = jnp.concatenate([take(w_gate, own), take(w_up, own)], axis=-1)
        own2 = take(w_down, own)
        got13, got2 = [], []
        for j, (pairs, send_to, _) in enumerate(routes):
            dst = jnp.asarray(np.array(send_to, np.int32))[me]
            idx = jnp.clip(place[:, dst * slots + j] - g * n_exp, 0, n_exp - 1)
            b13 = jnp.concatenate([take(w_gate, idx), take(w_up, idx)], axis=-1)
            b2 = take(w_down, idx)
            if pairs:
                b13 = lax.ppermute(b13, ("dp", "ep"), pairs)
                b2 = lax.ppermute(b2, ("dp", "ep"), pairs)
            got13.append(b13)
            got2.append(b2)
        local = jnp.asarray(np.array([r[2] for r in routes], bool).T)[me][None, :, None, None]
        w13 = jnp.where(local, own13, jnp.stack(got13, axis=1))
        w2 = jnp.where(local, own2, jnp.stack(got2, axis=1))
        return w13, w2

    spec_in = P(None, "ep", None, None)
    spec_out = P(None, ("dp", "ep"), None, None)
    return jax.shard_map(body, mesh=mesh,
                         in_specs=(spec_in, spec_in, spec_in, P(None, None)),
                         out_specs=(spec_out, spec_out), check_vma=False)
```

profile of v0, /device:TPU:0, one launch (start us, length us, event | category | flops | bytes accessed | tf_op | source)
XLA Modules:
  0.0 1358.2 jit_solution(3388005714893899165)
XLA Ops:
  7.1 33.9 %dynamic-slice_bitcast_fusion.4 = (bf16[1,4096,1536]{2,1,0:T(8,128)(2,1)}, bf16[1,4096,1536]{2,1,0:T(8,128)(2,1)}, bf16[1,4096,1536]{2,1,0:T(8,128)(2,1)}, bf16[1,4096,1536]{2,1,0:T(8,128)(2,1)}) fusion(bf16[1,2,4096,1536]{3,2,1,0:T(8,128)(2,1)} %param.8, s32[]{:T(128)} %bitcast.20, s32[]{:T(128)} %bitcast.27, bf16[1,2,4096,1536]{3,2,1,0:T(8,128)(2,1)} %param.7), kind=kLoop, calls=%fused_computation.29 | loop fusion | bytes 100663304 | tf_op jit(solution)/shard_map/vmap()/squeeze | solution.py:38
  40.9 20.9 %pad_maximum_fusion = bf16[1,4096,3072]{2,1,0:T(8,128)(2,1)} fusion(bf16[1,4096,1536]{2,1,0:T(8,128)(2,1)} %get-tuple-element.78, bf16[1,4096,1536]{2,1,0:T(8,128)(2,1)} %get-tuple-element.95), kind=kLoop, calls=%fused_computation.22 | loop fusion | flops 50331648 | bytes 50331648 | tf_op jit(solution)/shard_map/concatenate | solution.py:46
  66.4 20.9 %pad_maximum_fusion.1 = bf16[1,4096,3072]{2,1,0:T(8,128)(2,1)} fusion(bf16[1,4096,1536]{2,1,0:T(8,128)(2,1)} %get-tuple-element.79, bf16[1,4096,1536]{2,1,0:T(8,128)(2,1)} %get-tuple-element.94), kind=kLoop, calls=%fused_computation.23 | loop fusion | flops 50331648 | bytes 50331648 | tf_op jit(solution)/shard_map/concatenate | solution.py:46
  87.3 5.0 collective-permute-start.1
  92.3 17.4 %dynamic-slice_bitcast_fusion.1 = (bf16[1,1536,4096]{2,1,0:T(8,128)(2,1)}, bf16[1,1536,4096]{2,1,0:T(8,128)(2,1)}) fusion(bf16[1,2,1536,4096]{3,2,1,0:T(8,128)(2,1)} %param.9, s32[]{:T(128)} %bitcast.20, s32[]{:T(128)} %bitcast.27), kind=kLoop, calls=%fused_computation.26 | loop fusion | bytes 50331656 | tf_op jit(solution)/shard_map/vmap()/squeeze | solution.py:38
  111.6 11.1 collective-permute-start.3
  123.9 16.9 %fusion.5 = (bf16[1,2,640,1536]{3,2,1,0:T(8,128)(2,1)}, bf16[1,2,640,1536]{3,2,1,0:T(8,128)(2,1)}, bf16[1,2,640,1536]{3,2,1,0:T(8,128)(2,1)}, bf16[1,2,640,1536]...) fusion(bf16[1,2,4096,1536]{3,2,1,0:T(8,128)(2,1)} %param.7), kind=kLoop, calls=%fused_computation.64 | loop fusion | bytes 47185920 | tf_op jit(solution)/shard_map/vmap()/gather | solution.py:38
  169.7 17.0 %fusion.6 = (bf16[1,2,640,1536]{3,2,1,0:T(8,128)(2,1)}, bf16[1,2,640,1536]{3,2,1,0:T(8,128)(2,1)}, bf16[1,2,640,1536]{3,2,1,0:T(8,128)(2,1)}, bf16[1,2,640,1536]...) fusion(bf16[1,2,4096,1536]{3,2,1,0:T(8,128)(2,1)} %param.8), kind=kLoop, calls=%fused_computation.65 | loop fusion | bytes 47185920 | tf_op jit(solution)/shard_map/vmap()/gather | solution.py:38
  186.7 4.9 gather_fusion.7
  191.6 5.0 gather_fusion.8
  196.5 4.9 gather_fusion.9
  211.0 4.9 gather_fusion.12
  219.6 17.8 %fusion.4 = (bf16[1,2,1536,640]{3,2,1,0:T(8,128)(2,1)}, bf16[1,2,1536,640]{3,2,1,0:T(8,128)(2,1)}, bf16[1,2,1536,640]{3,2,1,0:T(8,128)(2,1)}, bf16[1,2,1536,640]...) fusion(bf16[1,2,1536,4096]{3,2,1,0:T(8,128)(2,1)} %param.9), kind=kLoop, calls=%fused_computation.63 | loop fusion | bytes 47185920 | tf_op jit(solution)/shard_map/vmap()/gather | solution.py:38
  237.3 5.0 gather_fusion.14
  242.4 5.0 gather_fusion.15
  247.4 5.2 gather_fusion.16
  252.6 5.0 gather_fusion.17
  257.6 5.1 gather_fusion.18
  262.7 5.1 gather_fusion.19
  287.2 8.1 bitcast_dynamic-update-slice_fusion.11
  335.0 406.6 %collective-permute-done.2 = bf16[1,1536,4096]{2,1,0:T(8,128)(2,1)} collective-permute-done((bf16[1,1536,4096]{2,1,0:T(8,128)(2,1)}, bf16[1,1536,4096]{2,1,0:T(8,128)(2,1)}, u32[]{:S(2)}, u32[]{:S(2)}) %collective-permute-start.2) | collective-permute-done | bytes 12582944 | tf_op jit(solution)/shard_map/ppermute | solution.py:50
  741.6 542.1 %collective-permute-done.3 = bf16[1,1536,4096]{2,1,0:T(8,128)(2,1)} collective-permute-done((bf16[1,1536,4096]{2,1,0:T(8,128)(2,1)}, bf16[1,1536,4096]{2,1,0:T(8,128)(2,1)}, u32[]{:S(2)}, u32[]{:S(2)}) %collective-permute-start.3) | collective-permute-done | bytes 12582944 | tf_op jit(solution)/shard_map/ppermute | solution.py:50
  1283.6 25.7 %maximum_select_fusion.1 = bf16[1,2,1536,4096]{3,2,1,0:T(8,128)(2,1)} fusion(bf16[1,2,1536,4096]{3,2,1,0:T(8,128)(2,1)} %copy-done, bf16[1,1,1536,4096]{3,2,1,0:T(8,128)(2,1)} %bitcast.41, bf16[1,1,1536,4096]{3,2,1,0:T(8,128)(2,1)} %bitcast.39, pred[2]{0:T(512)(128)(4,1)S(1)} %fusion), kind=kLoop, calls=%fused_computation.24 | loop fusion | flops 25165824 | bytes 75497472 | tf_op jit(solution)/shard_map/jit(_where)/select_n | solution.py:55
  1309.3 48.7 %maximum_select_fusion = bf16[1,2,4096,3072]{3,2,1,0:T(8,128)(2,1)} fusion(bf16[1,2,4096,1536]{3,2,1,0:T(8,128)(2,1)} %get-tuple-element.96, bf16[1,2,4096,1536]{3,2,1,0:T(8,128)(2,1)} %get-tuple-element.97, bf16[1,1,4096,3072]{3,2,1,0:T(8,128)(2,1)} %bitcast.30, bf16[1,1,4096,3072]{3,2,1,0:T(8,128)(2,1)} %bitcast.23, pred[2]{0:T(512)(128)(4,1)S(1)} %fusion), kind=kLoop, calls=%fused_computation.21 | loop fusion | flops 226492416 | bytes 150994944 | tf_op jit(solution)/shard_map/jit(_where)/select_n | solution.py:54
  (88 shorter events, 112.6 us)
Async XLA Ops:
  61.8 1247.5 %collective-permute-start = (bf16[1,4096,3072]{2,1,0:T(8,128)(2,1)}, bf16[1,4096,3072]{2,1,0:T(8,128)(2,1)}, u32[]{:S(2)}, u32[]{:S(2)}) collective-permute-start(bf16[1,4096,3072]{2,1,0:T(8,128)(2,1)} %pad_maximum_fusion), channel_id=1, source_target_pairs={{1,0},{2,1},{3,2},{0,3},{6,4},{4,6},{11,9},{9,11},{14,12},{12,14}} | collective-permute-start | bytes 75497480 | tf_op jit(solution)/shard_map/ppermute | solution.py:49
  87.3 1222.0 %collective-permute-start.1 = (bf16[1,4096,3072]{2,1,0:T(8,128)(2,1)}, bf16[1,4096,3072]{2,1,0:T(8,128)(2,1)}, u32[]{:S(2)}, u32[]{:S(2)}) collective-permute-start(bf16[1,4096,3072]{2,1,0:T(8,128)(2,1)} %pad_maximum_fusion.1), channel_id=1, source_target_pairs={{6,0},{7,1},{4,2},{5,3},{10,4},{11,5},{8,6},{9,7},{14,8},{15,9},{1... | collective-permute-start | bytes 75497480 | tf_op jit(solution)/shard_map/ppermute | solution.py:49
  109.7 631.9 %collective-permute-start.2 = (bf16[1,1536,4096]{2,1,0:T(8,128)(2,1)}, bf16[1,1536,4096]{2,1,0:T(8,128)(2,1)}, u32[]{:S(2)}, u32[]{:S(2)}) collective-permute-start(bf16[1,1536,4096]{2,1,0:T(8,128)(2,1)} %get-tuple-element.68), channel_id=1, source_target_pairs={{1,0},{2,1},{3,2},{0,3},{6,4},{4,6},{11,9},{9,11},{14,12},{12,14}} | collective-permute-start | bytes 37748744 | tf_op jit(solution)/shard_map/ppermute | solution.py:50
  111.6 1172.0 %collective-permute-start.3 = (bf16[1,1536,4096]{2,1,0:T(8,128)(2,1)}, bf16[1,1536,4096]{2,1,0:T(8,128)(2,1)}, u32[]{:S(2)}, u32[]{:S(2)}) collective-permute-start(bf16[1,1536,4096]{2,1,0:T(8,128)(2,1)} %get-tuple-element.69), channel_id=1, source_target_pairs={{6,0},{7,1},{4,2},{5,3},{10,4},{11,5},{8,6},{9,7},{14,8},{15,9},{1... | collective-permute-start | bytes 37748744 | tf_op jit(solution)/shard_map/ppermute | solution.py:50
  211.0 4.9 slice-start.1
  211.0 6.8 slice-start
  262.7 5.1 slice-start.2
  270.3 3.3 copy-start.16
  273.6 2.1 copy-start.15
  275.7 2.1 copy-start.14
  282.0 2.8 copy-start.6
  284.8 18.8 %copy-start = (bf16[1,2,1536,4096]{3,2,1,0:T(8,128)(2,1)}, bf16[1,2,1536,4096]{3,2,1,0:T(8,128)(2,1)S(1)}, u32[]{:S(2)}) copy-start(bf16[1,2,1536,4096]{3,2,1,0:T(8,128)(2,1)S(1)} %bitcast_dynamic-update-slice_fusion.18) | copy-start | bytes 75497472
  287.2 9.1 copy-start.5
  296.3 5.1 copy-start.4
  301.4 3.5 copy-start.3
  304.9 3.5 copy-start.1
  308.5 3.5 copy-start.2
  312.0 3.5 copy-start.11
  315.5 3.5 copy-start.10
  319.1 3.5 copy-start.9
  322.6 3.5 copy-start.7
  326.1 3.5 copy-start.8
  329.7 2.3 copy-start.17
  329.7 3.3 copy-start.18
  (3 other events, 4.9 us)
where the time goes:
time: 1360 us
  waiting for transfers between devices  949 us (70%)
  local copies, waits for them, and re-layouts  267 us (20%)
  other arithmetic  116 us (9%)
  starting transfers between devices  22.6 us (2%)
    ppermute x2, waiting for transfers between devices, body(): b2 = lax.ppermute(b2, ('dp', 'ep'), pairs)  949 us
    gather x31, local copies, waits for them, and re-layouts, body(): take = jax.vmap(lambda w, i: w[i])  146 us
    unnamed x61, local copies, waits for them, and re-layouts  65.3 us
    squeeze x2, local copies, waits for them, and re-layouts, body(): take = jax.vmap(lambda w, i: w[i])  51.3 us
    select_n x1, other arithmetic, body(): w13 = jnp.where(local, own13, jnp.stack(got13, axis=1))  48.7 us
    concatenate x2, other arithmetic, body(): b13 = jnp.concatenate([take(w_gate, idx), take(w_up, idx)], axis=-1)  41.8 us
  transfers between devices with their start and end apart: 4, of which 2 were waited for; matrix products, arithmetic and copies ran while one was open for 19% of the time, Pallas kernels for 0%

commit v1 on v0

v1 whole, which is shorter than its diff:
```python
import functools

import jax
import jax.numpy as jnp
from jax import lax
from jax.experimental import pallas as pl
from jax.experimental.pallas import tpu as pltpu
from jax.sharding import PartitionSpec as P

N = 64
NI = 4
NO = 8
LAG = 6
BUF_P, BUF_Q, BUF_R, BUF_S = range(4)
VMEM_LIMIT = 60 * 1024 * 1024


def _slot_of(place, a, g, j):
    return place[0, (a * 4 + g) * 2 + j] % 2


def _move(place, wg, wu, wd, sgu, sd, ig, og, idn, odn, ig2, og2, idn2, odn2, in_sem, out_sem, in2_sem, out2_sem, fwd_sem, recv_sem):
    total = 3 * N
    a = lax.axis_index("dp")
    g = lax.axis_index("ep")
    x, c = g // 2, g % 2
    rg, rd = wg.shape[2] // N, wd.shape[2] // N

    def dev(a2, c2, flip=False):
        return (a2, 2 * ((1 - x) if flip else x) + c2)

    def local(m, e, k):
        return wd.at[0, e, pl.ds(k * rd, rd)] if m == 2 else (wg, wu)[m].at[0, e, pl.ds(k * rg, rg)]

    def stage(m, b, k):
        return sd.at[b, pl.ds(k * rd, rd)] if m == 2 else sgu.at[b, m, pl.ds(k * rg, rg)]

    def stage_all(m, b):
        return sd.at[b] if m == 2 else sgu.at[b, m]

    def each(q, fn):
        for m in range(3):
            @pl.when((q >= m * N) & (q < (m + 1) * N))
            def _():
                fn(m, q - m * N)

    def remote(src, dst, ssem, rsem, device):
        return pltpu.make_async_remote_copy(src_ref=src, dst_ref=dst, send_sem=ssem, recv_sem=rsem, device_id=device,
                                            device_id_type=pl.DeviceIdType.MESH)

    here = (a, g)

    def wait_recv(b, q):
        each(q, lambda m, k: remote(stage(m, b, k), stage(m, b, k), fwd_sem.at[0, 0], recv_sem.at[b, q], dev(a, 1 - c)).wait_recv())

    def wait_all(b):
        def step(q, _):
            wait_recv(b, q)
            return 0
        lax.fori_loop(0, total, step, 0)

    def forward(q, b, flow, device):
        each(q, lambda m, k: remote(stage(m, b, k), stage(m, b, k), fwd_sem.at[flow, m], recv_sem.at[b, q], device).start())

    def wait_sent(flow, b, device):
        for m in range(3):
            remote(stage_all(m, b), stage_all(m, b), fwd_sem.at[flow, m], recv_sem.at[b, 0], device).wait_send()

    def pick_start(q, ins, sem, src0, src1):
        def go(m, k):
            buf = ins[m // 2].at[q % NI]
            pltpu.make_async_copy(src0(m, k), buf.at[0], sem.at[q % NI, 0]).start()
            pltpu.make_async_copy(src1(m, k), buf.at[1], sem.at[q % NI, 1]).start()
        each(q, go)

    def pick_run(q, ins, outs, sem, osem, src0, src1, which, b, device):
        def free(m, k):
            remote(outs[m // 2].at[q % NO], stage(m, b, k), osem.at[q % NO], recv_sem.at[b, 0], device).wait_send()
        each(jnp.where(q < total, q - NO, -1), free)

        def go(m, k):
            i, o = ins[m // 2], outs[m // 2]
            slot, oslot = q % NI, q % NO
            pltpu.make_async_copy(src0(m, k), i.at[slot, 0], sem.at[slot, 0]).wait()
            pltpu.make_async_copy(src1(m, k), i.at[slot, 1], sem.at[slot, 1]).wait()
            rows = 8 if m == 2 else 16

            def some(r, _):
                at = pl.ds(r * rows, rows)
                o[oslot, at] = jnp.where(which == 0, i[slot, 0, at], i[slot, 1, at])
                return 0
            lax.fori_loop(0, (rd if m == 2 else rg) // rows, some, 0)
        each(q, go)

    def pick_send(q, outs, osem, b, device):
        each(q, lambda m, k: remote(outs[m // 2].at[q % NO], stage(m, b, k), osem.at[q % NO], recv_sem.at[b, q], device).start())

    def pick_drain(outs, osem, b, device):
        def step(q, _):
            each(q, lambda m, k: remote(outs[m // 2].at[q % NO], stage(m, b, k), osem.at[q % NO], recv_sem.at[b, 0], device).wait_send())
            return 0
        lax.fori_loop(total - NO, total, step, 0)

    is_src = (c == 0) & (a < 2) | (c == 1) & (a >= 2)

    @pl.when(is_src)
    def _():
        other = 2 * (1 - x)
        a2 = _slot_of(place, 2, other, 1)
        b1 = _slot_of(place, 1, other + 1, 1)
        which = jnp.where(c == 0, a2, b1)
        which = jnp.where((a == 1) | (a == 2), 1 - which, which)
        b = a % 2
        mirror = (a, 2 * (1 - x) + c)
        src = (lambda m, k: local(m, 0, k)), (lambda m, k: local(m, 1, k))
        ins, outs = (ig, idn), (og, odn)
        b0 = _slot_of(place, 0, 2 * x + 1, 1) == _slot_of(place, 1, 2 * x + 1, 1)
        which2 = jnp.where(b0, 1, 0)
        src2 = (lambda m, k: stage(m, BUF_P, k)), (lambda m, k: stage(m, BUF_Q, k))
        ins2, outs2 = (ig2, idn2), (og2, odn2)
        to0 = dev(0, 1)

        def tick(t, _):
            pick_start(t, ins, in_sem, *src)
            pick_send(t - 3, outs, out_sem, b, mirror)
            pick_run(t - 2, ins, outs, in_sem, out_sem, *src, which, b, mirror)
            u = t - 3 - LAG
            wait_recv(b, u)

            @pl.when(a == 0)
            def _():
                forward(u, BUF_P, 0, dev(1, 0))
                forward(u, BUF_P, 1, dev(2, 0))
                forward(u, BUF_P, 2, dev(0, 1))

            @pl.when(a == 1)
            def _():
                forward(u, BUF_Q, 0, dev(0, 1))
                forward(u, BUF_Q, 1, dev(3, 0))

            @pl.when(a == 3)
            def _():
                forward(u, BUF_Q, 0, dev(2, 1))
                forward(u, BUF_Q, 1, dev(1, 1))

            @pl.when(a == 2)
            def _():
                wait_recv(BUF_Q, u)
                pick_start(u, ins2, in2_sem, *src2)
                pick_send(u - 3, outs2, out2_sem, BUF_R, to0)
                pick_run(u - 2, ins2, outs2, in2_sem, out2_sem, *src2, which2, BUF_R, to0)
            return 0
        lax.fori_loop(0, total + 3 + LAG + 3, tick, 0)
        pick_drain(outs, out_sem, b, mirror)

        @pl.when(a == 0)
        def _():
            wait_all(BUF_Q)
            wait_all(BUF_R)
            wait_all(BUF_S)
            wait_sent(0, BUF_P, dev(1, 0))
            wait_sent(1, BUF_P, dev(2, 0))
            wait_sent(2, BUF_P, dev(0, 1))

        @pl.when(a == 1)
        def _():
            wait_all(BUF_P)
            wait_sent(0, BUF_Q, dev(0, 1))
            wait_sent(1, BUF_Q, dev(3, 0))

        @pl.when(a == 3)
        def _():
            wait_sent(0, BUF_Q, dev(2, 1))
            wait_sent(1, BUF_Q, dev(1, 1))

        @pl.when(a == 2)
        def _():
            pick_drain(outs2, out2_sem, BUF_R, to0)

    @pl.when((a == 0) & (c == 1))
    def _():
        peer = dev(0, 0)

        def tick(q, _):
            def give(m, k):
                for e in range(2):
                    remote(local(m, e, k), stage(m, BUF_R + e, k), fwd_sem.at[1 + e, m], recv_sem.at[BUF_R + e, q], peer).start()
            each(q, give)
            wait_recv(BUF_Q, q)
            forward(q, BUF_Q, 0, peer)
            return 0
        lax.fori_loop(0, total, tick, 0)
        wait_all(BUF_P)
        wait_all(BUF_R)
        for flow, b in enumerate((BUF_Q, BUF_R, BUF_S)):
            wait_sent(flow, b, peer)

    @pl.when((a == 1) & (c == 1))
    def _():
        wait_all(BUF_Q)

    @pl.when((a == 2) & (c == 0))
    def _():
        def tick(q, _):
            wait_recv(BUF_P, q)
            forward(q, BUF_P, 0, dev(3, 0))
            return 0
        lax.fori_loop(0, total, tick, 0)
        wait_sent(0, BUF_P, dev(3, 0))

    @pl.when((a == 3) & (c == 0))
    def _():
        wait_all(BUF_P)
        wait_all(BUF_Q)


NP = 16
NB = 12
AHEAD = 6


def _place(place, wg, wu, wd, sgu, sd, w13, w2, bg, bd, in_sem, out_sem):
    a = lax.axis_index("dp")
    g = lax.axis_index("ep")
    x, c = g // 2, g % 2
    f = wg.shape[3]
    rg, rd = wg.shape[2] // NP, wd.shape[2] // NP

    a2 = _slot_of(place, 2, 2 * x, 1)
    b1 = _slot_of(place, 1, 2 * x + 1, 1)

    def source(j):
        e = _slot_of(place, a, g, j)
        far_a = jnp.where(e == a2, 2 + BUF_P, 2 + BUF_Q)
        far_b = jnp.where(e == b1, 2 + BUF_Q, 2 + BUF_P)
        if j == 0:
            c0 = jnp.where(a == 0, 2 + BUF_R + e, jnp.where(a == 2, e, far_a))
            c1 = jnp.where(a == 0, far_a, jnp.where(a == 2, far_b, e))
        else:
            c0 = far_a
            c1 = jnp.where(a == 0, 2 + BUF_R, jnp.where(a == 3, e, far_b))
        return jnp.where(c == 0, c0, c1)

    sources = [source(0), source(1)]

    def run(first, bufs, fetch, put):
        def tick(t, _):
            @pl.when(t < first)
            def _():
                slot = t % NB

                @pl.when(t >= NB)
                def _():
                    put(t - NB, slot, True)
                fetch(t, slot)
            u = t - AHEAD

            @pl.when(u >= 0)
            def _():
                slot = u % NB
                pltpu.make_async_copy(bufs.at[slot], bufs.at[slot], in_sem.at[slot]).wait()
                put(u, slot, False)
            return 0
        lax.fori_loop(0, first + AHEAD, tick, 0)

        def drain(t, _):
            put(t, t % NB, True)
            return 0
        lax.fori_loop(first - NB, first, drain, 0)

    def fetch_gu(t, slot):
        m, j, k = t // (2 * NP), (t // NP) % 2, t % NP
        s = jnp.where(j == 0, sources[0], sources[1])
        rows = pl.ds(k * rg, rg)
        for mm, w in enumerate((wg, wu)):
            @pl.when((s < 2) & (m == mm))
            def _():
                pltpu.make_async_copy(w.at[0, s, rows], bg.at[slot], in_sem.at[slot]).start()

        @pl.when(s >= 2)
        def _():
            pltpu.make_async_copy(sgu.at[s - 2, m, rows], bg.at[slot], in_sem.at[slot]).start()

    def put_gu(t, slot, wait):
        m, j, k = t // (2 * NP), (t // NP) % 2, t % NP
        for mm in range(2):
            @pl.when(m == mm)
            def _():
                cp = pltpu.make_async_copy(bg.at[slot], w13.at[0, j, pl.ds(k * rg, rg), pl.ds(mm * f, f)], out_sem.at[slot])
                cp.wait() if wait else cp.start()

    def fetch_d(t, slot):
        j, k = t // NP, t % NP
        s = jnp.where(j == 0, sources[0], sources[1])
        rows = pl.ds(k * rd, rd)

        @pl.when(s < 2)
        def _():
            pltpu.make_async_copy(wd.at[0, s, rows], bd.at[slot], in_sem.at[slot]).start()

        @pl.when(s >= 2)
        def _():
            pltpu.make_async_copy(sd.at[s - 2, rows], bd.at[slot], in_sem.at[slot]).start()

    def put_d(t, slot, wait):
        j, k = t // NP, t % NP
        cp = pltpu.make_async_copy(bd.at[slot], w2.at[0, j, pl.ds(k * rd, rd)], out_sem.at[slot])
        cp.wait() if wait else cp.start()

    run(4 * NP, bg, fetch_gu, put_gu)
    run(2 * NP, bd, fetch_d, put_d)


def solution(mesh):
    def body(w_gate, w_up, w_down, place):
        d, f = w_gate.shape[2], w_gate.shape[3]
        bf16 = w_gate.dtype
        hbm = pl.BlockSpec(memory_space=pl.ANY)
        smem = pl.BlockSpec(memory_space=pltpu.SMEM)
        rg, rd = d // N, f // N
        rings = [pltpu.VMEM((NI, 2, rg, f), bf16), pltpu.VMEM((NO, rg, f), bf16),
                 pltpu.VMEM((NI, 2, rd, d), bf16), pltpu.VMEM((NO, rd, d), bf16)]
        dma = pltpu.SemaphoreType.DMA
        sgu, sd = pl.pallas_call(
            _move,
            out_shape=(jax.ShapeDtypeStruct((4, 2, d, f), bf16), jax.ShapeDtypeStruct((4, f, d), bf16)),
            in_specs=[smem, hbm, hbm, hbm],
            out_specs=(hbm, hbm),
            scratch_shapes=rings + rings + [dma((NI, 2)), dma((NO,)), dma((NI, 2)), dma((NO,)), dma((3, 3)), dma((4, 3 * N))],
            compiler_params=pltpu.CompilerParams(has_side_effects=True, vmem_limit_bytes=VMEM_LIMIT),
            name="move",
        )(place, w_gate, w_up, w_down)
        return pl.pallas_call(
            _place,
            out_shape=(jax.ShapeDtypeStruct((1, 2, d, 2 * f), bf16), jax.ShapeDtypeStruct((1, 2, f, d), bf16)),
            in_specs=[smem] + [hbm] * 5,
            out_specs=(hbm, hbm),
            scratch_shapes=[pltpu.VMEM((NB, d // NP, f), bf16), pltpu.VMEM((NB, f // NP, d), bf16), dma((NB,)), dma((NB,))],
            compiler_params=pltpu.CompilerParams(vmem_limit_bytes=VMEM_LIMIT),
            name="place",
        )(place, w_gate, w_up, w_down, sgu, sd)

    spec_in = P(None, "ep", None, None)
    spec_out = P(None, ("dp", "ep"), None, None)
    return jax.shard_map(body, mesh=mesh,
                         in_specs=(spec_in, spec_in, spec_in, P(None, None)),
                         out_specs=(spec_out, spec_out), check_vma=False)
```

time: 1360 us -> 488 us (0.36)
  waiting for transfers between devices: 949 us -> 0 us
  Pallas kernels: 0 us -> 483 us
  local copies, waits for them, and re-layouts: 267 us -> 0 us
  other arithmetic: 116 us -> 0 us
  starting transfers between devices: 22.6 us -> 0 us
    ppermute x4 -> x0, waiting for transfers between devices: 949 us -> none  [the longest x2 949 us: body(): b2 = lax.ppermute(b2, ('dp', 'ep'), pairs)]
    pallas_call x0 -> x2, Pallas kernels: none -> 483 us  [the longest x1 432 us: body(): pl.pallas_call(_move, out_shape=(jax.ShapeDtypeStruct((4, 2, d, f), bf16)...]
    gather x31 -> x0, local copies, waits for them, and re-layouts: 146 us -> none  [body(): take = jax.vmap(lambda w, i: w[i])]
    select_n x2 -> x0, other arithmetic: 74.4 us -> none  [the longest x1 48.7 us: body(): w13 = jnp.where(local, own13, jnp.stack(got13, axis=1))]
    unnamed x61 -> x0, local copies, waits for them, and re-layouts: 65.3 us -> none
    squeeze x2 -> x0, local copies, waits for them, and re-layouts: 51.3 us -> none  [body(): take = jax.vmap(lambda w, i: w[i])]
    concatenate x2 -> x0, other arithmetic: 41.8 us -> none  [body(): b13 = jnp.concatenate([take(w_gate, idx), take(w_up, idx)], axis=-1)]
    ppermute x4 -> x0, starting transfers between devices: 22.6 us -> none  [the longest x2 13 us: body(): b2 = lax.ppermute(b2, ('dp', 'ep'), pairs)]
  transfers between devices with their start and end apart: 4 -> 0, of which waited for: 2 -> 0; matrix products, arithmetic and copies ran while one was open for 19% -> 0% of each run, Pallas kernels for 0% -> 0%
where the time goes in v1:
time: 488 us; the launch traced here: 484 us
  Pallas kernels  483 us (99%)
    pallas_call x1, Pallas kernels, body(): pl.pallas_call(_move, out_shape=(jax.ShapeDtypeStruct((4, 2, d, f), bf16)...  432 us
    pallas_call x1, Pallas kernels, body(): pl.pallas_call(_place, out_shape=(jax.ShapeDtypeStruct((1, 2, d, 2 * f),...  51.1 us

profile of v1, /device:TPU:0, one launch (start us, length us, event | category | flops | bytes accessed | tf_op | source)
XLA Modules:
  0.0 484.1 jit_solution(13190790341037273160)
XLA Ops:
  0.6 432.3 %move.1 = (bf16[4,2,4096,1536]{3,2,1,0:T(8,128)(2,1)}, bf16[4,1536,4096]{2,1,0:T(8,128)(2,1)}) custom-call(s32[1,32]{1,0:T(1,128)} %place.5, bf16[1,2,4096,1536]{3,2,1,0:T(8,128)(2,1)} %wg.3, bf16[1,2,4096,1536]{3,2,1,0:T(8,128)(2,1)} %wu.3, bf16[1,2,1536,4096]{3,2,1,0:T(8,128)(2,1)} %wd.3), custom_call_target="tpu_custom_call" | custom-call | tf_op jit(solution)/shard_map/move/pallas_call | solution.py:324
  433.0 51.1 %place.4 = (bf16[1,2,4096,3072]{3,2,1,0:T(8,128)(2,1)}, bf16[1,2,1536,4096]{3,2,1,0:T(8,128)(2,1)}) custom-call(s32[1,32]{1,0:T(1,128)} %place.5, bf16[1,2,4096,1536]{3,2,1,0:T(8,128)(2,1)} %wg.3, bf16[1,2,4096,1536]{3,2,1,0:T(8,128)(2,1)} %wu.3, bf16[1,2,1536,4096]{3,2,1,0:T(8,128)(2,1)} %wd.3, bf16[4,2,4096,1536]{3,2,1,0:T(8,128)(2,1)} %get-tuple-element.4.sgu, ...), custom_call_target="tpu_custom_call" | custom-call | tf_op jit(solution)/shard_map/place/pallas_call | solution.py:333

commit v2 on v0

v2 whole, which is shorter than its diff:
```python
import functools

import jax
import jax.numpy as jnp
from jax import lax
from jax.experimental import pallas as pl
from jax.experimental.pallas import tpu as pltpu
from jax.sharding import PartitionSpec as P

NG = 64
ND = 64
NI = 3
NO = 4
NI2 = 2
NV = 2
LAG = 4
LATE = 6
KEEP = 52
BUF_P, BUF_Q, BUF_R, BUF_S = range(4)
MOVE_VMEM = 11 * 1024 * 1024
PLACE_VMEM = 8 * 1024 * 1024


def _slot_of(place, a, g, j):
    return place[0, (a * 4 + g) * 2 + j] % 2


def _move(place, wg, wu, wd, sgu, sd, kup, kdn, ig, og, idn, odn, ig2, og2, idn2, odn2, vg, vd,
          in_sem, out_sem, in2_sem, out2_sem, v_sem, fwd_sem, recv_sem):
    total = 2 * NG + ND
    first = (0, NG, 2 * NG, total)
    a = lax.axis_index("dp")
    g = lax.axis_index("ep")
    x, c = g // 2, g % 2
    rg, rd = wg.shape[2] // NG, wd.shape[2] // ND

    def dev(a2, c2, flip=False):
        return (a2, 2 * ((1 - x) if flip else x) + c2)

    def local(m, e, k):
        return wd.at[0, e, pl.ds(k * rd, rd)] if m == 2 else (wg, wu)[m].at[0, e, pl.ds(k * rg, rg)]

    def stage(m, b, k):
        return sd.at[b, pl.ds(k * rd, rd)] if m == 2 else sgu.at[b, m, pl.ds(k * rg, rg)]

    def stage_all(m, b):
        return sd.at[b] if m == 2 else sgu.at[b, m]

    def each(q, fn):
        for m in range(3):
            @pl.when((q >= first[m]) & (q < first[m + 1]))
            def _():
                fn(m, q - first[m])

    def remote(src, dst, ssem, rsem, device):
        return pltpu.make_async_remote_copy(src_ref=src, dst_ref=dst, send_sem=ssem, recv_sem=rsem, device_id=device,
                                            device_id_type=pl.DeviceIdType.MESH)

    def wait_recv(b, q):
        each(q, lambda m, k: remote(stage(m, b, k), stage(m, b, k), fwd_sem.at[0, 0], recv_sem.at[b, q], dev(a, 1 - c)).wait_recv())

    def forward(q, b, flow, device):
        each(q, lambda m, k: remote(stage(m, b, k), stage(m, b, k), fwd_sem.at[flow, m], recv_sem.at[b, q], device).start())

    def wait_sent(flow, b, device):
        for m in range(3):
            remote(stage_all(m, b), stage_all(m, b), fwd_sem.at[flow, m], recv_sem.at[b, 0], device).wait_send()

    def pick_start(q, ins, sem, src0, src1):
        def go(m, k):
            buf = ins[m // 2].at[q % ins[0].shape[0]]
            pltpu.make_async_copy(src0(m, k), buf.at[0], sem.at[q % ins[0].shape[0], 0]).start()
            pltpu.make_async_copy(src1(m, k), buf.at[1], sem.at[q % ins[0].shape[0], 1]).start()
        each(q, go)

    def pick_run(q, ins, outs, sem, osem, src0, src1, which, b, device):
        def free(m, k):
            remote(outs[m // 2].at[q % NO], stage(m, b, k), osem.at[q % NO], recv_sem.at[b, 0], device).wait_send()
        each(jnp.where(q < total, q - NO, -1), free)

        def go(m, k):
            i, o = ins[m // 2], outs[m // 2]
            slot, oslot = q % i.shape[0], q % NO
            pltpu.make_async_copy(src0(m, k), i.at[slot, 0], sem.at[slot, 0]).wait()
            pltpu.make_async_copy(src1(m, k), i.at[slot, 1], sem.at[slot, 1]).wait()
            rows = 8 if m == 2 else 16

            def some(r, _):
                at = pl.ds(r * rows, rows)
                o[oslot, at] = jnp.where(which == 0, i[slot, 0, at], i[slot, 1, at])
                return 0
            lax.fori_loop(0, (rd if m == 2 else rg) // rows, some, 0)
        each(q, go)

    def pick_send(q, outs, osem, b, device):
        each(q, lambda m, k: remote(outs[m // 2].at[q % NO], stage(m, b, k), osem.at[q % NO], recv_sem.at[b, q], device).start())

    def pick_drain(outs, osem, b, device):
        def step(q, _):
            each(q, lambda m, k: remote(outs[m // 2].at[q % NO], stage(m, b, k), osem.at[q % NO], recv_sem.at[b, 0], device).wait_send())
            return 0
        lax.fori_loop(total - NO, total, step, 0)

    def greet(*partners):
        barrier = pltpu.get_barrier_semaphore()
        for device in partners:
            pl.semaphore_signal(barrier, inc=1, device_id=device, device_id_type=pl.DeviceIdType.MESH)
        pl.semaphore_wait(barrier, len(partners))

    mirror = (a, 2 * (1 - x) + c)
    for a2, c2, partners in (
        (0, 0, (mirror, dev(1, 0), dev(2, 0), dev(0, 1))),
        (0, 1, (dev(0, 0), dev(1, 0), dev(2, 1))),
        (1, 0, (mirror, dev(0, 0), dev(0, 1), dev(3, 0))),
        (1, 1, (dev(3, 1),)),
        (2, 0, (dev(0, 0), dev(3, 0))),
        (2, 1, (mirror, dev(3, 1), dev(0, 1))),
        (3, 0, (dev(1, 0), dev(2, 0))),
        (3, 1, (mirror, dev(2, 1), dev(1, 1))),
    ):
        pl.when((a == a2) & (c == c2))(functools.partial(greet, *partners))

    is_src = (c == 0) & (a < 2) | (c == 1) & (a >= 2)
    here = lambda a2, c2: (a == a2) & (c == c2)
    other = 2 * (1 - x)
    which = jnp.where(c == 0, _slot_of(place, 2, other, 1), _slot_of(place, 1, other + 1, 1))
    which = jnp.where((a == 1) | (a == 2), 1 - which, which)
    b = a % 2
    src = (lambda m, k: local(m, 0, k)), (lambda m, k: local(m, 1, k))
    ins, outs = (ig, idn), (og, odn)
    far_a, far_b = _slot_of(place, 2, 2 * x, 1), _slot_of(place, 1, 2 * x + 1, 1)
    which2 = jnp.where(_slot_of(place, 0, 2 * x + 1, 1) == far_b, 1, 0)
    src2 = (lambda m, k: stage(m, BUF_P, k)), (lambda m, k: stage(m, BUF_Q, k))
    ins2, outs2 = (ig2, idn2), (og2, odn2)
    to0 = dev(0, 1)
    flows = {
        (0, 0): (BUF_P, (dev(1, 0), dev(2, 0), dev(0, 1))),
        (0, 1): (BUF_Q, (dev(0, 0),)),
        (1, 0): (BUF_Q, (dev(0, 1), dev(3, 0))),
        (2, 0): (BUF_P, (dev(3, 0),)),
        (3, 1): (BUF_Q, (dev(2, 1), dev(1, 1))),
    }
    late = {(0, 0): (BUF_Q, BUF_R, BUF_S), (0, 1): (BUF_P, BUF_R), (1, 0): (BUF_P,), (1, 1): (BUF_Q,), (3, 0): (BUF_P, BUF_Q)}

    own = (here(1, 1) | here(2, 0) | here(3, 1), here(3, 1))
    pairs = ((jnp.where(here(0, 0), BUF_R, BUF_P), jnp.where(here(0, 0), BUF_S, BUF_Q)),
             (jnp.where(here(0, 1), BUF_R, jnp.where(here(1, 1), BUF_Q, BUF_P)),
              jnp.where(here(0, 1), BUF_R, jnp.where(here(2, 0), BUF_P, BUF_Q))))
    kept = []
    for j in range(2):
        e = _slot_of(place, a, g, j)
        from_a = (c == 0) | (here(0, 1) if j == 0 else False)
        far = jnp.where(from_a, jnp.where(e == far_a, 0, 1), jnp.where(e == far_b, 1, 0))
        kept.append(jnp.where(own[j] | (here(0, 0) if j == 0 else False), e, far))
    first_kept = 2 * NG - KEEP

    def keep_start(q):
        def go(m, k):
            for j in range(2):
                for e in range(2):
                    to, sem = (vg, vd)[m // 2].at[q % NV, j, e], v_sem.at[q % NV, j, e]

                    @pl.when(own[j])
                    def _():
                        pltpu.make_async_copy(local(m, e, k), to, sem).start()

                    @pl.when(jnp.logical_not(own[j]))
                    def _():
                        pltpu.make_async_copy(stage(m, pairs[j][e], k), to, sem).start()
        each(jnp.where(q < first_kept, -1, q), go)

    def keep_run(q):
        def go(m, k):
            v, o = ((vg, kup), (vd, kdn))[m // 2]
            n, rows = (rd, 8) if m == 2 else (rg, 16)
            base = k * rd if m == 2 else (k - (NG - KEEP)) * rg
            for j in range(2):
                for e in range(2):
                    pltpu.make_async_copy(local(m, e, k), v.at[q % NV, j, e], v_sem.at[q % NV, j, e]).wait()

                def some(r, _):
                    at = pl.ds(pl.multiple_of(r * rows, rows), rows)
                    o[j, pl.ds(pl.multiple_of(base + r * rows, rows), rows)] = jnp.where(kept[j] == 0, v[q % NV, j, 0, at], v[q % NV, j, 1, at])
                    return 0
                lax.fori_loop(0, n // rows, some, 0)
        each(jnp.where(q < first_kept, -1, q), go)

    def tick(t, _):
        u = t - 3 - LAG

        @pl.when(is_src)
        def _():
            pick_start(t, ins, in_sem, *src)
            pick_send(t - 3, outs, out_sem, b, mirror)
            pick_run(t - 2, ins, outs, in_sem, out_sem, *src, which, b, mirror)

        @pl.when(here(2, 1))
        def _():
            pick_send(u - 1, outs2, out2_sem, BUF_R, to0)
            wait_recv(BUF_P, u)
            wait_recv(BUF_Q, u)
            pick_start(u, ins2, in2_sem, *src2)
            pick_run(u, ins2, outs2, in2_sem, out2_sem, *src2, which2, BUF_R, to0)

        @pl.when(here(0, 1))
        def _():
            def give(m, k):
                for e in range(2):
                    remote(local(m, e, k), stage(m, BUF_R + e, k), fwd_sem.at[1 + e, m], recv_sem.at[BUF_R + e, t], dev(0, 0)).start()
            each(t, give)

        for (a2, c2), (block, devices) in flows.items():
            @pl.when(here(a2, c2))
            def _():
                wait_recv(block, u)
                for flow, device in enumerate(devices):
                    forward(u, block, flow, device)

        v = u - LATE
        for (a2, c2), blocks in late.items():
            @pl.when(here(a2, c2))
            def _():
                for block in blocks:
                    wait_recv(block, v)
        keep_start(v)
        keep_run(v - 1)
        return 0
    lax.fori_loop(0, total + 3 + LAG + LATE + 1, tick, 0)

    @pl.when(is_src)
    def _():
        pick_drain(outs, out_sem, b, mirror)

    @pl.when(here(2, 1))
    def _():
        pick_drain(outs2, out2_sem, BUF_R, to0)

    for (a2, c2), (block, devices) in flows.items():
        @pl.when(here(a2, c2))
        def _():
            for flow, device in enumerate(devices):
                wait_sent(flow, block, device)

    @pl.when(here(0, 1))
    def _():
        wait_sent(1, BUF_R, dev(0, 0))
        wait_sent(2, BUF_S, dev(0, 0))


NP = 32
NB = 14
AHEAD = 7
PARTS = 4


def _place(place, wg, wu, sgu, kup, kdn, w13, w2, bg, in_sem, out_sem, k_sem):
    a = lax.axis_index("dp")
    g = lax.axis_index("ep")
    x, c = g // 2, g % 2
    d, f = wg.shape[2], wg.shape[3]
    rows = d // NP
    nup = (d - kup.shape[1]) // rows
    total = 2 * (NP + nup)

    a2 = _slot_of(place, 2, 2 * x, 1)
    b1 = _slot_of(place, 1, 2 * x + 1, 1)

    def source(j):
        e = _slot_of(place, a, g, j)
        far_a = jnp.where(e == a2, 2 + BUF_P, 2 + BUF_Q)
        far_b = jnp.where(e == b1, 2 + BUF_Q, 2 + BUF_P)
        if j == 0:
            c0 = jnp.where(a == 0, 2 + BUF_R + e, jnp.where(a == 2, e, far_a))
            c1 = jnp.where(a == 0, far_a, jnp.where(a == 2, far_b, e))
        else:
            c0 = far_a
            c1 = jnp.where(a == 0, 2 + BUF_R, jnp.where(a == 3, e, jnp.where(a == 1, 2 + BUF_Q, far_b)))
        return jnp.where(c == 0, c0, c1)

    sources = [source(0), source(1)]

    def where(t):
        m = (t >= 2 * NP).astype(jnp.int32)
        r = t - m * 2 * NP
        n = jnp.where(m == 0, NP, nup)
        return m, r // n, r % n

    def fetch(t):
        slot = t % NB
        m, j, k = where(t)
        s = jnp.where(j == 0, sources[0], sources[1])
        at = pl.ds(k * rows, rows)
        for mm, w in enumerate((wg, wu)):
            @pl.when((s < 2) & (m == mm))
            def _():
                pltpu.make_async_copy(w.at[0, s, at], bg.at[slot], in_sem.at[slot]).start()

        @pl.when(s >= 2)
        def _():
            pltpu.make_async_copy(sgu.at[s - 2, m, at], bg.at[slot], in_sem.at[slot]).start()

    def put(t, wait):
        slot = t % NB
        m, j, k = where(t)
        for mm in range(2):
            @pl.when(m == mm)
            def _():
                cp = pltpu.make_async_copy(bg.at[slot], w13.at[0, j, pl.ds(k * rows, rows), pl.ds(mm * f, f)], out_sem.at[slot])
                cp.wait() if wait else cp.start()

    def kept():
        for j in range(2):
            for p in range(PARTS):
                n = kdn.shape[1] // PARTS
                at = pl.ds(p * n, n)
                yield pltpu.make_async_copy(kdn.at[j, at], w2.at[0, j, at], k_sem.at[0, j, p])
                n = kup.shape[1] // PARTS
                yield pltpu.make_async_copy(kup.at[j, pl.ds(p * n, n)], w13.at[0, j, pl.ds(nup * rows + p * n, n), pl.ds(f, f)], k_sem.at[1, j, p])

    def tick(t, _):
        @pl.when(t < total)
        def _():
            @pl.when(t >= NB)
            def _():
                put(t - NB, True)
            fetch(t)

        @pl.when(t == AHEAD - 1)
        def _():
            for cp in kept():
                cp.start()
        u = t - AHEAD

        @pl.when(u >= 0)
        def _():
            slot = u % NB
            pltpu.make_async_copy(bg.at[slot], bg.at[slot], in_sem.at[slot]).wait()
            put(u, False)
        return 0
    lax.fori_loop(0, total + AHEAD, tick, 0)

    def drain(t, _):
        put(t, True)
        return 0
    lax.fori_loop(total - NB, total, drain, 0)
    for cp in kept():
        cp.wait()


def solution(mesh):
    def body(w_gate, w_up, w_down, place):
        d, f = w_gate.shape[2], w_gate.shape[3]
        bf16 = w_gate.dtype
        hbm = pl.BlockSpec(memory_space=pltpu.HBM)
        smem = pl.BlockSpec(memory_space=pltpu.SMEM)
        kept = pl.BlockSpec(memory_space=pltpu.VMEM)
        rg, rd = d // NG, f // ND
        in_hbm = functools.partial(pltpu.with_memory_space_constraint, memory_space=pltpu.HBM)
        vmem, dma = pltpu.VMEM, pltpu.SemaphoreType.DMA
        sgu, sd, kup, kdn = pl.pallas_call(
            _move,
            out_shape=(jax.ShapeDtypeStruct((4, 2, d, f), bf16), jax.ShapeDtypeStruct((4, f, d), bf16),
                       vmem((2, KEEP * rg, f), bf16), vmem((2, f, d), bf16)),
            in_specs=[smem, hbm, hbm, hbm],
            out_specs=(hbm, hbm, kept, kept),
            scratch_shapes=[vmem((NI, 2, rg, f), bf16), vmem((NO, rg, f), bf16), vmem((NI, 2, rd, d), bf16), vmem((NO, rd, d), bf16),
                            vmem((NI2, 2, rg, f), bf16), vmem((NO, rg, f), bf16), vmem((NI2, 2, rd, d), bf16), vmem((NO, rd, d), bf16),
                            vmem((NV, 2, 2, rg, f), bf16), vmem((NV, 2, 2, rd, d), bf16),
                            dma((NI, 2)), dma((NO,)), dma((NI2, 2)), dma((NO,)), dma((NV, 2, 2)), dma((3, 3)), dma((4, 2 * NG + ND))],
            compiler_params=pltpu.CompilerParams(collective_id=0, has_side_effects=True, vmem_limit_bytes=MOVE_VMEM),
            name="move",
        )(place, in_hbm(w_gate), in_hbm(w_up), in_hbm(w_down))
        return pl.pallas_call(
            _place,
            out_shape=(jax.ShapeDtypeStruct((1, 2, d, 2 * f), bf16), jax.ShapeDtypeStruct((1, 2, f, d), bf16)),
            in_specs=[smem, hbm, hbm, hbm, kept, kept],
            out_specs=(hbm, hbm),
            scratch_shapes=[vmem((NB, d // NP, f), bf16), dma((NB,)), dma((NB,)), dma((2, 2, PARTS))],
            compiler_params=pltpu.CompilerParams(vmem_limit_bytes=PLACE_VMEM),
            name="place",
        )(place, in_hbm(w_gate), in_hbm(w_up), in_hbm(sgu), kup, kdn)

    spec_in = P(None, "ep", None, None)
    spec_out = P(None, ("dp", "ep"), None, None)
    return jax.shard_map(body, mesh=mesh,
                         in_specs=(spec_in, spec_in, spec_in, P(None, None)),
                         out_specs=(spec_out, spec_out), check_vma=False)
```

time: 1360 us -> 471 us (0.35)
  waiting for transfers between devices: 949 us -> 0 us
  Pallas kernels: 0 us -> 463 us
  local copies, waits for them, and re-layouts: 267 us -> 0.01 us
  other arithmetic: 116 us -> 0 us
  starting transfers between devices: 22.6 us -> 0 us
    ppermute x4 -> x0, waiting for transfers between devices: 949 us -> none  [the longest x2 949 us: body(): b2 = lax.ppermute(b2, ('dp', 'ep'), pairs)]
    pallas_call x0 -> x2, Pallas kernels: none -> 463 us  [the longest x1 428 us: body(): pl.pallas_call(_move, out_shape=(jax.ShapeDtypeStruct((4, 2, d, f), bf16)...]
    gather x31 -> x0, local copies, waits for them, and re-layouts: 146 us -> none  [body(): take = jax.vmap(lambda w, i: w[i])]
    select_n x2 -> x0, other arithmetic: 74.4 us -> none  [the longest x1 48.7 us: body(): w13 = jnp.where(local, own13, jnp.stack(got13, axis=1))]
    unnamed x61 -> x2, local copies, waits for them, and re-layouts: 65.3 us -> 0.01 us
    squeeze x2 -> x0, local copies, waits for them, and re-layouts: 51.3 us -> none  [body(): take = jax.vmap(lambda w, i: w[i])]
    concatenate x2 -> x0, other arithmetic: 41.8 us -> none  [body(): b13 = jnp.concatenate([take(w_gate, idx), take(w_up, idx)], axis=-1)]
    ppermute x4 -> x0, starting transfers between devices: 22.6 us -> none  [the longest x2 13 us: body(): b2 = lax.ppermute(b2, ('dp', 'ep'), pairs)]
  transfers between devices with their start and end apart: 4 -> 0, of which waited for: 2 -> 0; matrix products, arithmetic and copies ran while one was open for 19% -> 0% of each run, Pallas kernels for 0% -> 0%
where the time goes in v2:
time: 471 us; the launch traced here: 463 us
  Pallas kernels  463 us (98%)
    pallas_call x1, Pallas kernels, body(): pl.pallas_call(_move, out_shape=(jax.ShapeDtypeStruct((4, 2, d, f), bf16)...  428 us
    pallas_call x1, Pallas kernels, body(): pl.pallas_call(_place, out_shape=(jax.ShapeDtypeStruct((1, 2, d, 2 * f),...  35 us

profile of v2, /device:TPU:0, one launch (start us, length us, event | category | flops | bytes accessed | tf_op | source)
XLA Modules:
  0.0 463.2 jit_solution(16659565851056150092)
XLA Ops:
  0.6 0.0 copy-start
  0.6 427.6 %move.1 = (bf16[4,2,4096,1536]{3,2,1,0:T(8,128)(2,1)}, bf16[4,1536,4096]{2,1,0:T(8,128)(2,1)}, bf16[2,3328,1536]{2,1,0:T(8,128)(2,1)S(1)}, bf16[2,1536,4096]{2,1,0:T(8,128)(2,1)S(1)}) custom-call(s32[1,32]{1,0:T(1,128)} %place.5, bf16[1,2,4096,1536]{3,2,1,0:T(8,128)(2,1)} %wg.3, bf16[1,2,4096,1536]{3,2,1,0:T(8,128)(2,1)} %wu.3, bf16[1,2,1536,4096]{3,2,1,0:T(8,128)(2,1)} %wd.1), custom_call_target="tpu_custom_call" | custom-call | tf_op jit(solution)/shard_map/move/pallas_call | solution.py:360
  428.3 0.0 copy-done
  428.3 35.0 %place.4 = (bf16[1,2,4096,3072]{3,2,1,0:T(8,128)(2,1)}, bf16[1,2,1536,4096]{3,2,1,0:T(8,128)(2,1)}) custom-call(s32[1,32]{1,0:T(1,128)S(1)} %copy-done, bf16[1,2,4096,1536]{3,2,1,0:T(8,128)(2,1)} %wg.3, bf16[1,2,4096,1536]{3,2,1,0:T(8,128)(2,1)} %wu.3, bf16[4,2,4096,1536]{3,2,1,0:T(8,128)(2,1)} %get-tuple-element.5.sgu, ...), custom_call_target="tpu_custom_call" | custom-call | tf_op jit(solution)/shard_map/place/pallas_call | solution.py:373
Async XLA Ops:
  0.6 427.6 %copy-start = (s32[1,32]{1,0:T(1,128)S(1)}, s32[1,32]{1,0:T(1,128)}, u32[]{:S(2)}) copy-start(s32[1,32]{1,0:T(1,128)} %place.5) | copy-start | bytes 388

commit v3 on v0

v3 whole, which is shorter than its diff:
```python
import functools

import jax
import jax.numpy as jnp
from jax import lax
from jax.experimental import pallas as pl
from jax.experimental.pallas import tpu as pltpu
from jax.sharding import PartitionSpec as P

C = 8
NI = 3
NO = 4
NV = 3
LAG = 4
LATE = ((4, 3), (3, 0), (0, 0), (0, 0))
DIRECT = 3
DELAY1 = 2
DELAY3 = 0
FIRST_KEPT = 72
BUF_P, BUF_Q, BUF_R, BUF_S = range(4)
MOVE_VMEM = 8 * 1024 * 1024
PLACE_VMEM = 8 * 1024 * 1024
STEP = 2


def _slot_of(place, a, g, j):
    return place[0, (a * 4 + g) * 2 + j] % 2


def _move(place, wg, wu, wd, st, kv0, kv1, i1, o1, i2, o2, ring, i1_sem, o1_sem, i2_sem, o2_sem, k_sem, fwd_sem, recv_sem):
    kv = (kv0, kv1)
    tiles = wg.shape[1]
    per = tiles // C
    total = 3 * per
    a = lax.axis_index("dp")
    g = lax.axis_index("ep")
    x, c = g // 2, g % 2

    def here(a2, c2):
        return (a == a2) & (c == c2)

    def dev(a2, c2):
        return (a2, 2 * x + c2)

    def within(q, fn, lo=0, hi=total):
        pl.when((q >= lo) & (q < hi))(fn)

    def local(q, fn, lo=0):
        for m, w in enumerate((wg, wu, wd)):
            within(q, lambda w=w, m=m: fn(lambda e: w.at[e, pl.ds((q - m * per) * C, C)]), jnp.maximum(lo, m * per), (m + 1) * per)

    def stage(b, q):
        return st.at[b, pl.ds(q * C, C)]

    def remote(src, dst, ssem, rsem, device):
        return pltpu.make_async_remote_copy(src_ref=src, dst_ref=dst, send_sem=ssem, recv_sem=rsem, device_id=device,
                                            device_id_type=pl.DeviceIdType.MESH)

    def wait_recv(b, q):
        within(q, lambda: remote(stage(b, q), stage(b, q), fwd_sem.at[0, 0], recv_sem.at[b, q], dev(a, 1 - c)).wait_recv())

    def forward(q, b, flow, device, hi=total):
        within(q, lambda: remote(stage(b, q), stage(b, q), fwd_sem.at[flow, q // per], recv_sem.at[b, q], device).start(), 0, hi)

    def wait_sent(flow, b, device, hi=total):
        for m in range(3):
            at = pl.ds(m * tiles, min(tiles, hi * C - m * tiles))
            remote(st.at[b, at], st.at[b, at], fwd_sem.at[flow, m], recv_sem.at[b, 0], device).wait_send()

    def pick_run(q, i, o, i_sem, o_sem, which, b, device, lo, hi):
        slot, oslot = q % NI, q % NO

        def free():
            remote(o.at[oslot], stage(b, q), o_sem.at[oslot], recv_sem.at[b, 0], device).wait_send()
        within(q, free, lo + NO, hi)

        def go():
            for e in range(2):
                pltpu.make_async_copy(st.at[0, pl.ds(0, C)], i.at[slot, e], i_sem.at[slot, e]).wait()

            def some(r, _):
                at = pl.ds(r * STEP, STEP)
                o[oslot, at] = jnp.where(which == 0, i[slot, 0, at], i[slot, 1, at])
                return 0
            lax.fori_loop(0, C // STEP, some, 0)
        within(q, go, lo, hi)

    def pick_send(q, o, o_sem, b, device, lo, hi):
        within(q, lambda: remote(o.at[q % NO], stage(b, q), o_sem.at[q % NO], recv_sem.at[b, q], device).start(), lo, hi)

    def pick_drain(o, o_sem, b, device, lo, hi):
        for n in range(NO):
            q = hi - NO + n
            within(q, lambda: remote(o.at[q % NO], stage(b, q), o_sem.at[q % NO], recv_sem.at[b, 0], device).wait_send(), lo, hi)

    mirror = (a, 2 * (1 - x) + c)
    other = 2 * (1 - x)
    far = _slot_of(place, 2, other, 1), _slot_of(place, 1, other + 1, 1)
    which = jnp.where(c == 0, far[0], far[1])
    which = jnp.where(here(1, 0) | here(2, 1), 1 - which, which)
    which = jnp.where(here(0, 1), _slot_of(place, 0, other + 1, 1), which)
    is_src = (c == 0) & (a < 2) | (c == 1) & (a >= 2)
    lo = jnp.where(is_src, 0, jnp.where(here(0, 1) | here(3, 0), total - DIRECT, total))
    delay = jnp.where(is_src, 0, jnp.where(c == 1, DELAY1, DELAY3))
    b = jnp.where(is_src, a % 2, jnp.where(c == 1, BUF_R, BUF_P))

    def pick_start(q):
        def go(src):
            for e in range(2):
                pltpu.make_async_copy(src(e), i1.at[q % NI, e], i1_sem.at[q % NI, e]).start()
        local(q, go, lo)

    def pick(q):
        pick_run(q, i1, o1, i1_sem, o1_sem, which, b, mirror, lo, total)

    far_a, far_b = _slot_of(place, 2, 2 * x, 1), _slot_of(place, 1, 2 * x + 1, 1)
    which2 = jnp.where(_slot_of(place, 0, 2 * x + 1, 1) == far_b, 1, 0)
    short = total - DIRECT

    def second(u):
        pick_run(u - 1, i2, o2, i2_sem, o2_sem, which2, BUF_R, dev(0, 1), 0, short)
        wait_recv(BUF_P, u)
        wait_recv(BUF_Q, u)

        def go():
            for e, block in enumerate((BUF_P, BUF_Q)):
                pltpu.make_async_copy(stage(block, u), i2.at[u % NI, e], i2_sem.at[u % NI, e]).start()
        within(u, go, 0, short)
        pick_send(u - 1, o2, o2_sem, BUF_R, dev(0, 1), 0, short)

    flows = {
        (0, 0): (BUF_P, ((dev(1, 0), total), (dev(2, 0), total), (dev(0, 1), total))),
        (0, 1): (BUF_Q, ((dev(0, 0), total),)),
        (1, 0): (BUF_Q, ((dev(0, 1), total), (dev(3, 0), total))),
        (2, 0): (BUF_P, ((dev(3, 0), short),)),
        (3, 1): (BUF_Q, ((dev(2, 1), total), (dev(1, 1), total))),
    }
    late = {(0, 0): (BUF_Q, BUF_R, BUF_S), (0, 1): (BUF_P, BUF_R), (1, 0): (BUF_P,), (1, 1): (BUF_Q,), (3, 0): (BUF_P, BUF_Q)}

    own = (here(1, 1) | here(2, 0) | here(3, 1), here(3, 1))
    pairs = ((jnp.where(here(0, 0), BUF_R, BUF_P), jnp.where(here(0, 0), BUF_S, BUF_Q)),
             (jnp.where(here(0, 1), BUF_R, jnp.where(here(1, 1), BUF_Q, BUF_P)),
              jnp.where(here(0, 1), BUF_R, jnp.where(here(2, 0), BUF_P, BUF_Q))))
    kept = []
    for j in range(2):
        e = _slot_of(place, a, g, j)
        from_a = (c == 0) | (here(0, 1) if j == 0 else False)
        near = own[j] | (here(0, 0) if j == 0 else False)
        kept.append(jnp.where(near, e, jnp.where(from_a, jnp.where(e == far_a, 0, 1), jnp.where(e == far_b, 1, 0))))

    def keep_to(q, j, e):
        return kv[j].at[pl.ds((q - FIRST_KEPT) * C, C)] if e == 0 else ring.at[q % NV, j]

    def keep_start(q):
        for j in range(2):
            def fetch(src, j=j):
                for e in range(2):
                    pltpu.make_async_copy(src(e), keep_to(q, j, e), k_sem.at[q % NV, j, e]).start()

            @pl.when(own[j])
            def _():
                local(q, fetch, FIRST_KEPT)

            @pl.when(jnp.logical_not(own[j]))
            def _():
                within(q, lambda: fetch(lambda e: stage(pairs[j][e], q)), FIRST_KEPT)

    def keep_run(q):
        def go():
            for j in range(2):
                for e in range(2):
                    pltpu.make_async_copy(st.at[0, pl.ds(0, C)], keep_to(q, j, e), k_sem.at[q % NV, j, e]).wait()

                def some(r, _):
                    at = pl.ds((q - FIRST_KEPT) * C + r * STEP, STEP)
                    kv[j][at] = jnp.where(kept[j] == 0, kv[j][at], ring[q % NV, j, pl.ds(r * STEP, STEP)])
                    return 0
                lax.fori_loop(0, C // STEP, some, 0)
        within(q, go, FIRST_KEPT)

    barrier = pltpu.get_barrier_semaphore()

    def greet(*partners):
        for device in partners:
            pl.semaphore_signal(barrier, inc=1, device_id=device, device_id_type=pl.DeviceIdType.MESH)

    partners = {
        (0, 0): (mirror, dev(1, 0), dev(2, 0), dev(0, 1)),
        (0, 1): (mirror, dev(0, 0), dev(1, 0), dev(2, 1)),
        (1, 0): (mirror, dev(0, 0), dev(0, 1), dev(3, 0)),
        (1, 1): (dev(3, 1),),
        (2, 0): (dev(0, 0), dev(3, 0)),
        (2, 1): (mirror, dev(3, 1), dev(0, 1)),
        (3, 0): (mirror, dev(1, 0), dev(2, 0)),
        (3, 1): (mirror, dev(2, 1), dev(1, 1)),
    }
    for (a2, c2), devices in partners.items():
        pl.when(here(a2, c2))(functools.partial(greet, *devices))

    def early(t, _):
        pick_start(t - delay)
        return 0
    lax.fori_loop(0, 3, early, 0)
    pick(0 - delay)
    for (a2, c2), devices in partners.items():
        pl.when(here(a2, c2))(lambda devices=devices: pl.semaphore_wait(barrier, len(devices)))

    behind = jnp.int32(0)
    for a2, cores in enumerate(LATE):
        for c2, n in enumerate(cores):
            behind = jnp.where(here(a2, c2), n, behind)

    def tick(t, _):
        u = t - 3 - LAG
        pick_send(t - 3 - delay, o1, o1_sem, b, mirror, lo, total)
        pick_start(t - delay)
        pick(t - 2 - delay)

        @pl.when(here(0, 1))
        def _():
            q = t - 3

            def give(src):
                for e in range(2):
                    remote(src(e), stage(BUF_R + e, q), fwd_sem.at[1 + e, q // per], recv_sem.at[BUF_R + e, q], dev(0, 0)).start()
            local(q, give)

        @pl.when(here(2, 1))
        def _():
            second(u)

        for (a2, c2), (block, devices) in flows.items():
            @pl.when(here(a2, c2))
            def _():
                wait_recv(block, u)
                for flow, (device, hi) in enumerate(devices):
                    forward(u, block, flow, device, hi)

        v = u - behind
        for (a2, c2), blocks in late.items():
            @pl.when(here(a2, c2))
            def _():
                for block in blocks:
                    wait_recv(block, v)
        keep_start(v)
        keep_run(v - 2)
        return 0
    lax.fori_loop(3, total + 3 + LAG + max(map(max, LATE)) + 2, tick, 0)

    pick_drain(o1, o1_sem, b, mirror, lo, total)

    @pl.when(here(2, 1))
    def _():
        pick_drain(o2, o2_sem, BUF_R, dev(0, 1), 0, short)

    for (a2, c2), (block, devices) in flows.items():
        @pl.when(here(a2, c2))
        def _():
            for flow, (device, hi) in enumerate(devices):
                wait_sent(flow, block, device, hi)

    @pl.when(here(0, 1))
    def _():
        wait_sent(1, BUF_R, dev(0, 0))
        wait_sent(2, BUF_S, dev(0, 0))


T = 32
NB = 8
AHEAD = 4
PARTS = 4
SPREAD = 2


def _place(place, wg, wu, st, kv0, kv1, w13, w2, buf, in_sem, out_sem, k_sem):
    kv = (kv0, kv1)
    a = lax.axis_index("dp")
    g = lax.axis_index("ep")
    x, c = g // 2, g % 2
    tiles = wg.shape[1]
    wide = w13.shape[2] // 2
    rest = FIRST_KEPT * C
    n = rest // T
    total = 2 * n

    far_a, far_b = _slot_of(place, 2, 2 * x, 1), _slot_of(place, 1, 2 * x + 1, 1)

    def source(j):
        e = _slot_of(place, a, g, j)
        from_a = jnp.where(e == far_a, 2 + BUF_P, 2 + BUF_Q)
        from_b = jnp.where(e == far_b, 2 + BUF_Q, 2 + BUF_P)
        if j == 0:
            c0 = jnp.where(a == 0, 2 + BUF_R + e, jnp.where(a == 2, e, from_a))
            c1 = jnp.where(a == 0, from_a, jnp.where(a == 2, from_b, e))
        else:
            c0 = jnp.where(a == 2, 2 + BUF_P, from_a)
            c1 = jnp.where(a == 0, 2 + BUF_R, jnp.where(a == 3, e, jnp.where(a == 1, 2 + BUF_Q, from_b)))
        return jnp.where(c == 0, c0, c1)

    sources = [source(0), source(1)]

    def fetch(t):
        slot = t % NB
        s = jnp.where(t % 2 == 0, sources[0], sources[1])
        k = t // 2
        m = k * T // tiles
        for mm, w in enumerate((wg, wu)):
            @pl.when((s < 2) & (m == mm))
            def _():
                pltpu.make_async_copy(w.at[s, pl.ds(k * T - mm * tiles, T)], buf.at[slot], in_sem.at[slot]).start()

        @pl.when(s >= 2)
        def _():
            pltpu.make_async_copy(st.at[s - 2, pl.ds(k * T, T)], buf.at[slot], in_sem.at[slot]).start()

    def put(t):
        k = t // 2
        m = k * T // tiles
        return pltpu.make_async_copy(buf.at[t % NB], w13.at[t % 2, pl.ds(k * T - m * tiles, T), pl.ds(m * wide, wide)], out_sem.at[t % NB])

    def kept():
        for j in range(2):
            for m in range(2):
                low, high = max(rest, m * tiles), (m + 1) * tiles
                step = T * max(1, (high - low) // T // PARTS)
                for p, at in enumerate(range(low, high, step)):
                    size = min(step, high - at)
                    yield pltpu.make_async_copy(kv[j].at[pl.ds(at - rest, size)],
                                                w13.at[j, pl.ds(at - m * tiles, size), pl.ds(m * wide, wide)], k_sem.at[m, j, p])
            step = tiles // PARTS
            for p in range(PARTS):
                yield pltpu.make_async_copy(kv[j].at[pl.ds(2 * tiles - rest + p * step, step)], w2.at[j, pl.ds(p * step, step)], k_sem.at[2, j, p])

    def tick(t, _):
        @pl.when(t < total)
        def _():
            @pl.when(t >= NB)
            def _():
                put(t - NB).wait()
            fetch(t)

        for n, cp in enumerate(kept()):
            pl.when(t == AHEAD - 1 + n * SPREAD)(cp.start)
        u = t - AHEAD

        @pl.when(u >= 0)
        def _():
            slot = u % NB
            pltpu.make_async_copy(st.at[0, pl.ds(0, T)], buf.at[slot], in_sem.at[slot]).wait()
            put(u).start()
        return 0
    lax.fori_loop(0, total + AHEAD, tick, 0)

    def drain(t, _):
        put(t).wait()
        return 0
    lax.fori_loop(total - NB, total, drain, 0)
    for cp in kept():
        cp.wait()


def _tiles(w, wide):
    _, e, r, k = w.shape
    return w.reshape(e, r // 8, 8, k // 128, 128).transpose(0, 1, 3, 2, 4).reshape(e, -1, wide, 8, 128)


def solution(mesh):
    def body(w_gate, w_up, w_down, place):
        d, f = w_gate.shape[2], w_gate.shape[3]
        bf16 = w_gate.dtype
        wg, wu, wd = (pltpu.with_memory_space_constraint(_tiles(w, f // 128), pltpu.HBM) for w in (w_gate, w_up, w_down))
        tiles, row = wg.shape[1], wg.shape[2:]
        hbm = pl.BlockSpec(memory_space=pltpu.HBM)
        smem = pl.BlockSpec(memory_space=pltpu.SMEM)
        kept = pl.BlockSpec(memory_space=pltpu.VMEM)
        vmem, dma = pltpu.VMEM, pltpu.SemaphoreType.DMA
        shape = jax.ShapeDtypeStruct
        keep = vmem((3 * tiles - FIRST_KEPT * C, *row), bf16)
        st, kv0, kv1 = pl.pallas_call(
            _move,
            out_shape=(shape((4, 3 * tiles, *row), bf16), keep, keep),
            in_specs=[smem, hbm, hbm, hbm],
            out_specs=(hbm, kept, kept),
            scratch_shapes=[vmem((NI, 2, C, *row), bf16), vmem((NO, C, *row), bf16), vmem((NI, 2, C, *row), bf16),
                            vmem((NO, C, *row), bf16), vmem((NV, 2, C, *row), bf16), dma((NI, 2)), dma((NO,)), dma((NI, 2)),
                            dma((NO,)), dma((NV, 2, 2)), dma((3, 3)), dma((4, 3 * tiles // C))],
            compiler_params=pltpu.CompilerParams(collective_id=0, has_side_effects=True, vmem_limit_bytes=MOVE_VMEM),
            name="move",
        )(place, wg, wu, wd)
        w13, w2 = pl.pallas_call(
            _place,
            out_shape=(shape((2, d // 8, f // 64, 8, 128), bf16), shape((2, tiles, *row), bf16)),
            in_specs=[smem, hbm, hbm, hbm, kept, kept],
            out_specs=(hbm, hbm),
            scratch_shapes=[vmem((NB, T, *row), bf16), dma((NB,)), dma((NB,)), dma((3, 2, 2 * PARTS))],
            compiler_params=pltpu.CompilerParams(vmem_limit_bytes=PLACE_VMEM),
            name="place",
        )(place, wg, wu, pltpu.with_memory_space_constraint(st, pltpu.HBM), kv0, kv1)
        w13 = w13.transpose(0, 1, 3, 2, 4).reshape(1, 2, d, 2 * f)
        w2 = w2.reshape(2, f // 8, d // 128, 8, 128).transpose(0, 1, 3, 2, 4).reshape(1, 2, f, d)
        return w13, w2

    spec_in = P(None, "ep", None, None)
    spec_out = P(None, ("dp", "ep"), None, None)
    return jax.shard_map(body, mesh=mesh,
                         in_specs=(spec_in, spec_in, spec_in, P(None, None)),
                         out_specs=(spec_out, spec_out), check_vma=False)
```

time: 1360 us -> 466 us (0.34)
  waiting for transfers between devices: 949 us -> 0 us
  Pallas kernels: 0 us -> 461 us
  local copies, waits for them, and re-layouts: 267 us -> 0.65 us
  other arithmetic: 116 us -> 0 us
  starting transfers between devices: 22.6 us -> 0 us
    ppermute x4 -> x0, waiting for transfers between devices: 949 us -> none  [the longest x2 949 us: body(): b2 = lax.ppermute(b2, ('dp', 'ep'), pairs)]
    pallas_call x0 -> x2, Pallas kernels: none -> 461 us  [the longest x1 426 us: body(): pl.pallas_call(_move, out_shape=(shape((4, 3 * tiles, *row), bf16), keep,...]
    gather x31 -> x0, local copies, waits for them, and re-layouts: 146 us -> none  [body(): take = jax.vmap(lambda w, i: w[i])]
    select_n x2 -> x0, other arithmetic: 74.4 us -> none  [the longest x1 48.7 us: body(): w13 = jnp.where(local, own13, jnp.stack(got13, axis=1))]
    unnamed x61 -> x2, local copies, waits for them, and re-layouts: 65.3 us -> 0.65 us
    squeeze x2 -> x0, local copies, waits for them, and re-layouts: 51.3 us -> none  [body(): take = jax.vmap(lambda w, i: w[i])]
    concatenate x2 -> x0, other arithmetic: 41.8 us -> none  [body(): b13 = jnp.concatenate([take(w_gate, idx), take(w_up, idx)], axis=-1)]
    ppermute x4 -> x0, starting transfers between devices: 22.6 us -> none  [the longest x2 13 us: body(): b2 = lax.ppermute(b2, ('dp', 'ep'), pairs)]
  transfers between devices with their start and end apart: 4 -> 0, of which waited for: 2 -> 0; matrix products, arithmetic and copies ran while one was open for 19% -> 0% of each run, Pallas kernels for 0% -> 0%
where the time goes in v3:
time: 466 us; the launch traced here: 462 us
  Pallas kernels  461 us (99%)
    pallas_call x1, Pallas kernels, body(): pl.pallas_call(_move, out_shape=(shape((4, 3 * tiles, *row), bf16), keep,...  426 us
    pallas_call x1, Pallas kernels, body(): pl.pallas_call(_place, out_shape=(shape((2, d // 8, f // 64, 8, 128), bf1...  34.4 us

profile of v3, /device:TPU:0, one launch (start us, length us, event | category | flops | bytes accessed | tf_op | source)
XLA Modules:
  0.0 462.0 jit_solution(10575834132613203397)
XLA Ops:
  0.6 0.0 copy-start
  0.6 0.6 copy-done
  1.3 426.2 %move.1 = (bf16[4,1536,12,8,128]{4,3,2,1,0:T(8,128)(2,1)}, bf16[960,12,8,128]{3,2,1,0:T(8,128)(2,1)S(1)}, bf16[960,12,8,128]{3,2,1,0:T(8,128)(2,1)S(1)}) custom-call(s32[1,32]{1,0:T(1,128)S(1)} %copy-done, bf16[2,512,12,8,128]{4,3,2,1,0:T(8,128)(2,1)} %bitcast.19, bf16[2,512,12,8,128]{4,3,2,1,0:T(8,128)(2,1)} %bitcast.21, bf16[2,512,12,8,128]{4,3,2,1,0:T(8,128)(2,1)} %bitcast.23), custom_call_target="tpu_custom_call" | custom-call | tf_op jit(solution)/shard_map/move/pallas_call | solution.py:379
  427.5 34.4 %place.4 = (bf16[2,512,24,8,128]{4,3,2,1,0:T(8,128)(2,1)}, bf16[2,512,12,8,128]{4,3,2,1,0:T(8,128)(2,1)}) custom-call(s32[1,32]{1,0:T(1,128)S(1)} %copy-done, bf16[2,512,12,8,128]{4,3,2,1,0:T(8,128)(2,1)} %bitcast.20, bf16[2,512,12,8,128]{4,3,2,1,0:T(8,128)(2,1)} %bitcast.22, bf16[4,1536,12,8,128]{4,3,2,1,0:T(8,128)(2,1)} %get-tuple-element.7.st, ...), custom_call_target="tpu_custom_call" | custom-call | tf_op jit(solution)/shard_map/place/pallas_call | solution.py:390
Async XLA Ops:
  0.6 0.7 copy-start

commit v4 on v3

--- a/solution.py
+++ b/solution.py
@@ -118,15 +118,15 @@
     short = total - DIRECT
 
     def second(u):
-        pick_run(u - 1, i2, o2, i2_sem, o2_sem, which2, BUF_R, dev(0, 1), 0, short)
+        pick_send(u - 2, o2, o2_sem, BUF_R, dev(0, 1), 0, short)
         wait_recv(BUF_P, u)
         wait_recv(BUF_Q, u)
+        pick_run(u - 1, i2, o2, i2_sem, o2_sem, which2, BUF_R, dev(0, 1), 0, short)
 
         def go():
             for e, block in enumerate((BUF_P, BUF_Q)):
                 pltpu.make_async_copy(stage(block, u), i2.at[u % NI, e], i2_sem.at[u % NI, e]).start()
         within(u, go, 0, short)
-        pick_send(u - 1, o2, o2_sem, BUF_R, dev(0, 1), 0, short)
 
     flows = {
         (0, 0): (BUF_P, ((dev(1, 0), total), (dev(2, 0), total), (dev(0, 1), total))),

time: 466 us -> 462 us (level)
  no operation moved by 1% of the time
where the time goes in v4:
time: 462 us
  Pallas kernels  461 us (100%)
    pallas_call x1, Pallas kernels, body(): pl.pallas_call(_move, out_shape=(shape((4, 3 * tiles, *row), bf16), keep,...  426 us
    pallas_call x1, Pallas kernels, body(): pl.pallas_call(_place, out_shape=(shape((2, d // 8, f // 64, 8, 128), bf1...  34.4 us

profile of v4, /device:TPU:0, one launch (start us, length us, event | category | flops | bytes accessed | tf_op | source)
XLA Modules:
  0.0 462.0 jit_solution(10713840572529564159)
XLA Ops:
  0.6 0.0 copy-start
  0.6 0.6 copy-done
  1.3 426.2 %move.1 = (bf16[4,1536,12,8,128]{4,3,2,1,0:T(8,128)(2,1)}, bf16[960,12,8,128]{3,2,1,0:T(8,128)(2,1)S(1)}, bf16[960,12,8,128]{3,2,1,0:T(8,128)(2,1)S(1)}) custom-call(s32[1,32]{1,0:T(1,128)S(1)} %copy-done, bf16[2,512,12,8,128]{4,3,2,1,0:T(8,128)(2,1)} %bitcast.19, bf16[2,512,12,8,128]{4,3,2,1,0:T(8,128)(2,1)} %bitcast.21, bf16[2,512,12,8,128]{4,3,2,1,0:T(8,128)(2,1)} %bitcast.23), custom_call_target="tpu_custom_call" | custom-call | tf_op jit(solution)/shard_map/move/pallas_call | solution.py:379
  427.5 34.4 %place.4 = (bf16[2,512,24,8,128]{4,3,2,1,0:T(8,128)(2,1)}, bf16[2,512,12,8,128]{4,3,2,1,0:T(8,128)(2,1)}) custom-call(s32[1,32]{1,0:T(1,128)S(1)} %copy-done, bf16[2,512,12,8,128]{4,3,2,1,0:T(8,128)(2,1)} %bitcast.20, bf16[2,512,12,8,128]{4,3,2,1,0:T(8,128)(2,1)} %bitcast.22, bf16[4,1536,12,8,128]{4,3,2,1,0:T(8,128)(2,1)} %get-tuple-element.7.st, ...), custom_call_target="tpu_custom_call" | custom-call | tf_op jit(solution)/shard_map/place/pallas_call | solution.py:390
Async XLA Ops:
  0.6 0.7 copy-start

commit v5 on v4

--- a/solution.py
+++ b/solution.py
@@ -16,7 +16,8 @@
 DIRECT = 3
 DELAY1 = 2
 DELAY3 = 0
-FIRST_KEPT = 72
+FIRST_KEPT = 68
+LAST = 4
 BUF_P, BUF_Q, BUF_R, BUF_S = range(4)
 MOVE_VMEM = 8 * 1024 * 1024
 PLACE_VMEM = 8 * 1024 * 1024
@@ -159,11 +160,11 @@
 
             @pl.when(own[j])
             def _():
-                local(q, fetch, FIRST_KEPT)
+                local(jnp.where(q < total - LAST, q, -1), fetch, FIRST_KEPT)
 
             @pl.when(jnp.logical_not(own[j]))
             def _():
-                within(q, lambda: fetch(lambda e: stage(pairs[j][e], q)), FIRST_KEPT)
+                within(q, lambda: fetch(lambda e: stage(pairs[j][e], q)), FIRST_KEPT, total - LAST)
 
     def keep_run(q):
         def go():
@@ -176,7 +177,7 @@
                     kv[j][at] = jnp.where(kept[j] == 0, kv[j][at], ring[q % NV, j, pl.ds(r * STEP, STEP)])
                     return 0
                 lax.fori_loop(0, C // STEP, some, 0)
-        within(q, go, FIRST_KEPT)
+        within(q, go, FIRST_KEPT, total - LAST)
 
     barrier = pltpu.get_barrier_semaphore()
 
@@ -245,7 +246,7 @@
         keep_start(v)
         keep_run(v - 2)
         return 0
-    lax.fori_loop(3, total + 3 + LAG + max(map(max, LATE)) + 2, tick, 0)
+    lax.fori_loop(3, total + 3 + LAG + max(map(max, LATE)), tick, 0)
 
     pick_drain(o1, o1_sem, b, mirror, lo, total)
 
@@ -272,7 +273,7 @@
 SPREAD = 2
 
 
-def _place(place, wg, wu, st, kv0, kv1, w13, w2, buf, in_sem, out_sem, k_sem):
+def _place(place, wg, wu, wd, st, kv0, kv1, w13, w2, buf, in_sem, out_sem, k_sem):
     kv = (kv0, kv1)
     a = lax.axis_index("dp")
     g = lax.axis_index("ep")
@@ -280,8 +281,9 @@
     tiles = wg.shape[1]
     wide = w13.shape[2] // 2
     rest = FIRST_KEPT * C
+    end = 3 * tiles - LAST * C
     n = rest // T
-    total = 2 * n
+    total = 2 * (n + 1)
 
     far_a, far_b = _slot_of(place, 2, 2 * x, 1), _slot_of(place, 1, 2 * x + 1, 1)
 
@@ -303,20 +305,31 @@
         slot = t % NB
         s = jnp.where(t % 2 == 0, sources[0], sources[1])
         k = t // 2
-        m = k * T // tiles
-        for mm, w in enumerate((wg, wu)):
+        low = jnp.where(k < n, k * T, end)
+        m = low // tiles
+        for mm, w in enumerate((wg, wu, wd)):
             @pl.when((s < 2) & (m == mm))
             def _():
-                pltpu.make_async_copy(w.at[s, pl.ds(k * T - mm * tiles, T)], buf.at[slot], in_sem.at[slot]).start()
+                pltpu.make_async_copy(w.at[s, pl.ds(low - mm * tiles, T)], buf.at[slot], in_sem.at[slot]).start()
 
         @pl.when(s >= 2)
         def _():
-            pltpu.make_async_copy(st.at[s - 2, pl.ds(k * T, T)], buf.at[slot], in_sem.at[slot]).start()
-
-    def put(t):
+            pltpu.make_async_copy(st.at[s - 2, pl.ds(low, T)], buf.at[slot], in_sem.at[slot]).start()
+
+    def put(t, wait):
         k = t // 2
         m = k * T // tiles
-        return pltpu.make_async_copy(buf.at[t % NB], w13.at[t % 2, pl.ds(k * T - m * tiles, T), pl.ds(m * wide, wide)], out_sem.at[t % NB])
+        src, sem = buf.at[t % NB], out_sem.at[t % NB]
+
+        @pl.when(k < n)
+        def _():
+            cp = pltpu.make_async_copy(src, w13.at[t % 2, pl.ds(k * T - m * tiles, T), pl.ds(m * wide, wide)], sem)
+            cp.wait() if wait else cp.start()
+
+        @pl.when(k == n)
+        def _():
+            cp = pltpu.make_async_copy(src, w2.at[t % 2, pl.ds(end - 2 * tiles, T)], sem)
+            cp.wait() if wait else cp.start()
 
     def kept():
         for j in range(2):
@@ -329,14 +342,15 @@
                                                 w13.at[j, pl.ds(at - m * tiles, size), pl.ds(m * wide, wide)], k_sem.at[m, j, p])
             step = tiles // PARTS
             for p in range(PARTS):
-                yield pltpu.make_async_copy(kv[j].at[pl.ds(2 * tiles - rest + p * step, step)], w2.at[j, pl.ds(p * step, step)], k_sem.at[2, j, p])
+                size = min(step, end - 2 * tiles - p * step)
+                yield pltpu.make_async_copy(kv[j].at[pl.ds(2 * tiles - rest + p * step, size)], w2.at[j, pl.ds(p * step, size)], k_sem.at[2, j, p])
 
     def tick(t, _):
         @pl.when(t < total)
         def _():
             @pl.when(t >= NB)
             def _():
-                put(t - NB).wait()
+                put(t - NB, True)
             fetch(t)
 
         for n, cp in enumerate(kept()):
@@ -347,12 +361,12 @@
         def _():
             slot = u % NB
             pltpu.make_async_copy(st.at[0, pl.ds(0, T)], buf.at[slot], in_sem.at[slot]).wait()
-            put(u).start()
+            put(u, False)
         return 0
     lax.fori_loop(0, total + AHEAD, tick, 0)
 
     def drain(t, _):
-        put(t).wait()
+        put(t, True)
         return 0
     lax.fori_loop(total - NB, total, drain, 0)
     for cp in kept():
@@ -375,7 +389,7 @@
         kept = pl.BlockSpec(memory_space=pltpu.VMEM)
         vmem, dma = pltpu.VMEM, pltpu.SemaphoreType.DMA
         shape = jax.ShapeDtypeStruct
-        keep = vmem((3 * tiles - FIRST_KEPT * C, *row), bf16)
+        keep = vmem((3 * tiles - (FIRST_KEPT + LAST) * C, *row), bf16)
         st, kv0, kv1 = pl.pallas_call(
             _move,
             out_shape=(shape((4, 3 * tiles, *row), bf16), keep, keep),
@@ -390,12 +404,12 @@
         w13, w2 = pl.pallas_call(
             _place,
             out_shape=(shape((2, d // 8, f // 64, 8, 128), bf16), shape((2, tiles, *row), bf16)),
-            in_specs=[smem, hbm, hbm, hbm, kept, kept],
+            in_specs=[smem, hbm, hbm, hbm, hbm, kept, kept],
             out_specs=(hbm, hbm),
             scratch_shapes=[vmem((NB, T, *row), bf16), dma((NB,)), dma((NB,)), dma((3, 2, 2 * PARTS))],
             compiler_params=pltpu.CompilerParams(vmem_limit_bytes=PLACE_VMEM),
             name="place",
-        )(place, wg, wu, pltpu.with_memory_space_constraint(st, pltpu.HBM), kv0, kv1)
+        )(place, wg, wu, wd, pltpu.with_memory_space_constraint(st, pltpu.HBM), kv0, kv1)
         w13 = w13.transpose(0, 1, 3, 2, 4).reshape(1, 2, d, 2 * f)
         w2 = w2.reshape(2, f // 8, d // 128, 8, 128).transpose(0, 1, 3, 2, 4).reshape(1, 2, f, d)
         return w13, w2

time: 462 us -> 461 us (level)
  no operation moved by 1% of the time
where the time goes in v5:
time: 461 us
  Pallas kernels  459 us (100%)
    pallas_call x1, Pallas kernels, body(): pl.pallas_call(_move, out_shape=(shape((4, 3 * tiles, *row), bf16), keep,...  425 us
    pallas_call x1, Pallas kernels, body(): pl.pallas_call(_place, out_shape=(shape((2, d // 8, f // 64, 8, 128), bf1...  34.4 us

profile of v5, /device:TPU:0, one launch (start us, length us, event | category | flops | bytes accessed | tf_op | source)
XLA Modules:
  0.0 460.6 jit_solution(3037427764120113313)
XLA Ops:
  0.6 0.0 copy-start
  0.6 0.6 copy-done
  1.3 424.9 %move.1 = (bf16[4,1536,12,8,128]{4,3,2,1,0:T(8,128)(2,1)}, bf16[960,12,8,128]{3,2,1,0:T(8,128)(2,1)S(1)}, bf16[960,12,8,128]{3,2,1,0:T(8,128)(2,1)S(1)}) custom-call(s32[1,32]{1,0:T(1,128)S(1)} %copy-done, bf16[2,512,12,8,128]{4,3,2,1,0:T(8,128)(2,1)} %bitcast.19, bf16[2,512,12,8,128]{4,3,2,1,0:T(8,128)(2,1)} %bitcast.21, bf16[2,512,12,8,128]{4,3,2,1,0:T(8,128)(2,1)} %bitcast.23), custom_call_target="tpu_custom_call" | custom-call | tf_op jit(solution)/shard_map/move/pallas_call | solution.py:393
  426.2 34.4 %place.4 = (bf16[2,512,24,8,128]{4,3,2,1,0:T(8,128)(2,1)}, bf16[2,512,12,8,128]{4,3,2,1,0:T(8,128)(2,1)}) custom-call(s32[1,32]{1,0:T(1,128)S(1)} %copy-done, bf16[2,512,12,8,128]{4,3,2,1,0:T(8,128)(2,1)} %bitcast.20, bf16[2,512,12,8,128]{4,3,2,1,0:T(8,128)(2,1)} %bitcast.22, bf16[2,512,12,8,128]{4,3,2,1,0:T(8,128)(2,1)} %bitcast.24, ...), custom_call_target="tpu_custom_call" | custom-call | tf_op jit(solution)/shard_map/place/pallas_call | solution.py:404
Async XLA Ops:
  0.6 0.7 copy-start

commit v6 on v5

--- a/solution.py
+++ b/solution.py
@@ -16,11 +16,11 @@
 DIRECT = 3
 DELAY1 = 2
 DELAY3 = 0
-FIRST_KEPT = 68
+FIRST_KEPT = 64
 LAST = 4
 BUF_P, BUF_Q, BUF_R, BUF_S = range(4)
-MOVE_VMEM = 8 * 1024 * 1024
-PLACE_VMEM = 8 * 1024 * 1024
+MOVE_VMEM = 7 * 1024 * 1024
+PLACE_VMEM = 7 * 1024 * 1024
 STEP = 2
 
 

time: 461 us -> 460 us (level)
  no operation moved by 1% of the time
where the time goes in v6:
time: 460 us
  Pallas kernels  459 us (100%)
    pallas_call x1, Pallas kernels, body(): pl.pallas_call(_move, out_shape=(shape((4, 3 * tiles, *row), bf16), keep,...  425 us
    pallas_call x1, Pallas kernels, body(): pl.pallas_call(_place, out_shape=(shape((2, d // 8, f // 64, 8, 128), bf1...  33.9 us

profile of v6, /device:TPU:0, one launch (start us, length us, event | category | flops | bytes accessed | tf_op | source)
XLA Modules:
  0.0 460.1 jit_solution(432953894871259483)
XLA Ops:
  0.6 0.0 copy-start
  0.6 0.6 copy-done
  1.3 424.9 %move.1 = (bf16[4,1536,12,8,128]{4,3,2,1,0:T(8,128)(2,1)}, bf16[992,12,8,128]{3,2,1,0:T(8,128)(2,1)S(1)}, bf16[992,12,8,128]{3,2,1,0:T(8,128)(2,1)S(1)}) custom-call(s32[1,32]{1,0:T(1,128)S(1)} %copy-done, bf16[2,512,12,8,128]{4,3,2,1,0:T(8,128)(2,1)} %bitcast.19, bf16[2,512,12,8,128]{4,3,2,1,0:T(8,128)(2,1)} %bitcast.21, bf16[2,512,12,8,128]{4,3,2,1,0:T(8,128)(2,1)} %bitcast.23), custom_call_target="tpu_custom_call" | custom-call | tf_op jit(solution)/shard_map/move/pallas_call | solution.py:393
  426.2 33.9 %place.4 = (bf16[2,512,24,8,128]{4,3,2,1,0:T(8,128)(2,1)}, bf16[2,512,12,8,128]{4,3,2,1,0:T(8,128)(2,1)}) custom-call(s32[1,32]{1,0:T(1,128)S(1)} %copy-done, bf16[2,512,12,8,128]{4,3,2,1,0:T(8,128)(2,1)} %bitcast.20, bf16[2,512,12,8,128]{4,3,2,1,0:T(8,128)(2,1)} %bitcast.22, bf16[2,512,12,8,128]{4,3,2,1,0:T(8,128)(2,1)} %bitcast.24, ...), custom_call_target="tpu_custom_call" | custom-call | tf_op jit(solution)/shard_map/place/pallas_call | solution.py:404
Async XLA Ops:
  0.6 0.7 copy-start

commit v7 on v6

--- a/solution.py
+++ b/solution.py
@@ -354,7 +354,7 @@
             fetch(t)
 
         for n, cp in enumerate(kept()):
-            pl.when(t == AHEAD - 1 + n * SPREAD)(cp.start)
+            pl.when(t == AHEAD - 1 + n * SPREAD)(functools.partial(cp.start, priority=1))
         u = t - AHEAD
 
         @pl.when(u >= 0)

time: 460 us -> 460 us (level)
  no operation moved by 1% of the time
where the time goes in v7:
time: 460 us
  Pallas kernels  459 us (100%)
    pallas_call x1, Pallas kernels, body(): pl.pallas_call(_move, out_shape=(shape((4, 3 * tiles, *row), bf16), keep,...  425 us
    pallas_call x1, Pallas kernels, body(): pl.pallas_call(_place, out_shape=(shape((2, d // 8, f // 64, 8, 128), bf1...  33.8 us

profile of v7, /device:TPU:0, one launch (start us, length us, event | category | flops | bytes accessed | tf_op | source)
XLA Modules:
  0.0 460.0 jit_solution(14015337786934277845)
XLA Ops:
  0.6 0.0 copy-start
  0.6 0.6 copy-done
  1.3 424.9 %move.1 = (bf16[4,1536,12,8,128]{4,3,2,1,0:T(8,128)(2,1)}, bf16[992,12,8,128]{3,2,1,0:T(8,128)(2,1)S(1)}, bf16[992,12,8,128]{3,2,1,0:T(8,128)(2,1)S(1)}) custom-call(s32[1,32]{1,0:T(1,128)S(1)} %copy-done, bf16[2,512,12,8,128]{4,3,2,1,0:T(8,128)(2,1)} %bitcast.19, bf16[2,512,12,8,128]{4,3,2,1,0:T(8,128)(2,1)} %bitcast.21, bf16[2,512,12,8,128]{4,3,2,1,0:T(8,128)(2,1)} %bitcast.23), custom_call_target="tpu_custom_call" | custom-call | tf_op jit(solution)/shard_map/move/pallas_call | solution.py:393
  426.2 33.8 %place.4 = (bf16[2,512,24,8,128]{4,3,2,1,0:T(8,128)(2,1)}, bf16[2,512,12,8,128]{4,3,2,1,0:T(8,128)(2,1)}) custom-call(s32[1,32]{1,0:T(1,128)S(1)} %copy-done, bf16[2,512,12,8,128]{4,3,2,1,0:T(8,128)(2,1)} %bitcast.20, bf16[2,512,12,8,128]{4,3,2,1,0:T(8,128)(2,1)} %bitcast.22, bf16[2,512,12,8,128]{4,3,2,1,0:T(8,128)(2,1)} %bitcast.24, ...), custom_call_target="tpu_custom_call" | custom-call | tf_op jit(solution)/shard_map/place/pallas_call | solution.py:404
Async XLA Ops:
  0.6 0.7 copy-start
